TPU v7x, 128 devices: a whole 4x4x4 slice. The times are simulated.
128 devices in a mesh: row: 16 (over y, x_hi, core), col: 8 (over x_lo, z).
Axes of the slice: x: 4 (x_hi: 2, x_lo: 2; x = x_hi * 2 + x_lo), y: 4, z: 4, core: 2. Of those that a mesh axis runs over, the one named last changes fastest.
Arguments:
- matrix: float32 [8, 16, 128, 16, 8, 128], P(None, 'row', None, None, 'col'), may hold values from -6 to 6
- reflectors: float32 [16, 8, 128, 512], P(None, 'col'), as said below
Outputs:
- updated: float32 [8, 16, 128, 16, 8, 128], P(None, 'row', None, None, 'col')
Inputs may be any that keep to these rules, and one draw needn't show every extreme that they name: Read as a 16384 x 512 matrix, the columns of reflectors are orthonormal.
All inputs are finite; a program needn't handle non-finite values.
Results may differ from a plain program's by a relative error of at most 0.0001.
Values sent between devices are 32-bit elements; how exact they have to be, the bound alone decides.
A program may use at most 128 MiB of HBM per device.

v0:
```python
import jax
import jax.numpy as jnp
from jax import lax
from jax.sharding import PartitionSpec as P


def from_root(value, axis, source):
    kept = jnp.where(lax.axis_index(axis) == source, value, 0).astype(value.dtype)
    return lax.psum(kept, axis)


def rows_for(lines, peers):
    spare = -len(lines) % peers
    return jnp.pad(lines, [(0, spare)] + [(0, 0)] * (lines.ndim - 1))


def sum_by_parts(x, axis):
    lines = x.reshape(-1, *x.shape[1:][-1:])
    own = lax.psum_scatter(
        rows_for(lines, lax.axis_size(axis)), axis, scatter_dimension=0, tiled=True
    )
    whole = lax.all_gather(own, axis).reshape(-1, *lines.shape[1:])
    return lax.slice_in_dim(whole, 0, len(lines)).reshape(x.shape)


def per_device(matrix, reflectors):
    row_count = lax.axis_size("row")
    col_count = lax.axis_size("col")
    stride = row_count // col_count
    row_index = lax.axis_index("row")
    col_index = lax.axis_index("col")
    row_tiles, _, tile_size, col_tiles, _, _ = matrix.shape
    total_rank = reflectors.shape[3]
    local_rows = row_tiles * tile_size
    local_cols = col_tiles * tile_size
    current = matrix.reshape(local_rows, local_cols)
    row_ids = (
        (jnp.arange(row_tiles)[:, None] * row_count + row_index) * tile_size
        + jnp.arange(tile_size)[None, :]
    ).reshape(-1)
    col_ids = (
        (jnp.arange(col_tiles)[:, None] * col_count + col_index) * tile_size
        + jnp.arange(tile_size)[None, :]
    ).reshape(-1)
    lower_mask = row_ids[:, None] >= col_ids[None, :]
    strict_mask = row_ids[:, None] > col_ids[None, :]
    refl_cols = reflectors.reshape(local_cols, total_rank)

    def pick_rows(source):
        breadth = source.shape[1]
        blocks = source.reshape(row_tiles, stride, tile_size, breadth)
        chosen = lax.dynamic_index_in_dim(blocks, row_index // col_count, axis=1, keepdims=False)
        return chosen.reshape(local_rows, breadth)

    def matmul(left_side, right_side):
        return jnp.dot(
            left_side,
            right_side,
            precision=lax.Precision.HIGHEST,
            preferred_element_type=jnp.float32,
        )

    def inner(left_side, right_side):
        return lax.dot_general(
            left_side,
            right_side,
            (((0,), (0,)), ((), ())),
            precision=lax.Precision.HIGHEST,
            preferred_element_type=jnp.float32,
        )

    refl_rows = from_root(pick_rows(refl_cols), "col", row_index % col_count)
    direct_part = matmul(jnp.where(lower_mask, current, 0.0), refl_cols)
    trans_part = inner(jnp.where(strict_mask, current, 0.0), refl_rows)
    direct = lax.psum(direct_part, "col")
    transposed = sum_by_parts(trans_part, "row")
    w_rows = direct + from_root(pick_rows(transposed), "col", row_index % col_count)
    breadth = direct.shape[1]
    pieces = []
    for offset in range(stride):
        moved = from_root(direct, "row", col_index + offset * col_count)
        pieces.append(moved.reshape(row_tiles, tile_size, breadth))
    w_cols = transposed + jnp.stack(pieces, axis=1).reshape(local_cols, breadth)
    projection = lax.psum(inner(refl_rows, w_rows), "row")
    w_rows = w_rows - 0.5 * matmul(refl_rows, projection)
    w_cols = w_cols - 0.5 * matmul(refl_cols, projection)
    left_side = jnp.concatenate([refl_rows, w_rows], axis=1)
    right_side = jnp.concatenate([w_cols, refl_cols], axis=1)
    current = current - lax.dot_general(
        left_side,
        right_side,
        (((1,), (1,)), ((), ())),
        precision=lax.Precision.HIGHEST,
        preferred_element_type=jnp.float32,
    )
    return jnp.where(lower_mask, current, 0.0).reshape(matrix.shape)


def solution(mesh):
    placed = (P(None, "row", None, None, "col", None), P(None, "col", None, None))
    return jax.shard_map(
        per_device,
        mesh=mesh,
        in_specs=placed,
        out_specs=P(None, "row", None, None, "col", None),
        check_vma=False,
    )
```

profile of v0, /device:TPU:0, one launch (start us, length us, event | category | flops | bytes accessed | tf_op | source)
XLA Modules:
  0.0 595.8 jit_solution(9861063768099171922)
XLA Ops:
  6.5 3.2 bitcast_select_fusion.3
  9.9 0.1 iota_add_fusion.1
  9.9 0.1 iota_add_fusion
  10.0 84.9 %all-reduce.6.cloned.1.call-done = f32[1024,512]{1,0:T(8,128)} async-done(((f32[1024,512]{1,0:T(8,128)}), f32[1024,512]{1,0:T(8,128)}) %all-reduce.6.cloned.1.call-update) | async-done | bytes 2097168 | tf_op jit(solution)/shard_map/psum | solution.py:9
  94.9 19.6 %fusion.4 = f32[2048,512]{1,0:T(8,128)} fusion(f32[1024,512]{1,0:T(8,128)} %all-reduce.6.cloned.1.call-done, f32[128,8,16,128]{3,2,1,0:T(8,128)} %bitcast.60, s32[2048]{0:T(1024)S(1)} %get-tuple-element.16, s32[1024]{0:T(1024)S(1)} %get-tuple-element.14), kind=kOutput, calls=%fused_computation.7 | convolution fusion | flops 12889096192 | bytes 14692352 | tf_op jit(solution)/shard_map/dot_general | solution.py:64
  114.5 80.9 %reduce-scatter.2.cloned.1.call-done = f32[128,512]{1,0:T(8,128)} async-done(((f32[2048,512]{1,0:T(8,128)}), f32[128,512]{1,0:T(8,128)}) %reduce-scatter.2.cloned.1.call-update) | async-done | bytes 262160 | tf_op jit(solution)/shard_map/reduce_scatter | solution.py:19
  195.5 0.2 all-reduce.10.cloned.1.call-start
  195.7 32.2 %fusion = f32[8,128,16,128]{3,2,1,0:T(8,128)} fusion(f32[8,1,128,16,1,128]{5,4,3,2,1,0:T(1,128)} %param.2, s32[16,128]{1,0:T(8,128)S(1)} %get-tuple-element.15, s32[8,128]{1,0:T(8,128)S(1)} %get-tuple-element.13), kind=kLoop, calls=%fused_computation.1 | loop fusion | flops 4194304 | bytes 16789504 | tf_op jit(solution)/shard_map/jit(_where)/select_n | solution.py:73
  227.9 20.0 %fusion.1 = f32[1024,512]{1,0:T(8,128)} fusion(f32[2048,512]{1,0:T(8,128)S(1)} %bitcast.54, f32[128,8,16,128]{3,2,1,0:T(8,128)} %bitcast.64), kind=kOutput, calls=%fused_computation.2 | convolution fusion | flops 12884901888 | bytes 14680064 | tf_op jit(solution)/shard_map/dot_general | solution.py:56
  247.9 3.5 all-gather.3.cloned.1.call-done
  251.5 3.2 bitcast_select_fusion.2
  254.7 0.4 all-reduce.8.cloned.1.call-start
  255.2 103.2 %all-reduce.10.cloned.1.call-done = (f32[1024,512]{1,0:T(8,128)}, f32[1024,512]{1,0:T(8,128)}) async-done(((f32[1024,512]{1,0:T(8,128)}, f32[1024,512]{1,0:T(8,128)}), (f32[1024,512]{1,0:T(8,128)}, f32[1024,512]{1,0:T(8,128)})) %all-reduce.10.cloned.1.call-update) | async-done | bytes 4194320 | tf_op jit(solution)/shard_map/psum | solution.py:75
  358.4 5.4 fusion.27
  363.8 4.6 fusion.28
  368.4 161.3 %all-reduce.8.cloned.1.call-done = (f32[8,1,128,512]{3,2,0,1:T(8,128)}, f32[8,1,128,512]{3,2,0,1:T(8,128)}, f32[512,512]{1,0:T(8,128)}) async-done(((f32[8,1,128,512]{3,2,0,1:T(8,128)}, f32[8,1,128,512]{3,2,0,1:T(8,128)}, f32[512,512]{1,0:T(8,128)}), (f32[8,1,128,512]{3,2,0,1:T(8,128)}, f32[8,1,128,512]{3,2,0,1:T(8,128)}, f32[512,512]{1,0:T(8,128)})) %all-reduce.8.cloned.1.call-update) | async-done | bytes 5242896 | tf_op jit(solution)/shard_map/psum | solution.py:9
  529.8 2.7 pad_maximum_fusion
  532.5 0.6 copy.5
  533.1 0.9 copy-done.4
  534.1 0.3 copy-done.5
  534.3 4.8 multiply_subtract_fusion
  539.1 7.5 %bitcast_subtract_fusion.1 = f32[2048,512]{1,0:T(8,128)S(1)} fusion(f32[2048,512]{1,0:T(8,128)S(1)} %copy-done.2, f32[8,2,128,512]{3,2,1,0:T(8,128)S(1)} %copy.5, f32[512,512]{1,0:T(8,128)S(1)} %copy-done.5, f32[2048,512]{1,0:T(8,128)S(1)} %bitcast.55), kind=kOutput, calls=%fused_computation.20 | convolution fusion | flops 6445596672 | bytes 17825792 | tf_op jit(solution)/shard_map/dot_general | solution.py:56
  546.7 33.6 %fusion.6 = f32[128,8,16,128]{3,1,2,0:T(8,128)} fusion(f32[128,8,16,128]{3,2,1,0:T(8,128)S(1)} %bitcast.63, s32[2048]{0:T(1024)S(1)} %get-tuple-element.16, s32[1024]{0:T(1024)S(1)} %get-tuple-element.14, f32[2048,512]{1,0:T(8,128)S(1)} %bitcast.56, f32[2048,512]{1,0:T(8,128)S(1)} %bitcast_subtract_fusion.1, f32[1024,512]{1,0:T(8,128)S(1)} %copy-done.6, ...), kind=kOutput, calls=%fused_computation.9 | convolution fusion | flops 25779240960 | bytes 29372416 | tf_op jit(solution)/shard_map/dot_general | solution.py:89
  580.3 8.8 %copy.11 = f32[128,8,16,128]{3,2,1,0:T(8,128)} copy(f32[128,8,16,128]{3,1,2,0:T(8,128)} %fusion.6) | data formatting | bytes 16777216
  (27 shorter events, 0.2 us)
Async XLA Ops:
  6.5 88.4 %all-reduce.6.cloned.1.call-start = ((), (), s32[]{:S(2)}) async-start(), calls=%async_computation.1 | async-start | bytes 4194304 | tf_op jit(solution)/shard_map/psum | solution.py:9
  9.8 185.7 %reduce-scatter.2.cloned.1.call-start = ((), (), s32[]{:S(2)}) async-start(), calls=%async_computation.2 | async-start | bytes 4456448 | tf_op jit(solution)/shard_map/reduce_scatter | solution.py:19
  114.5 137.0 %all-gather.3.cloned.1.call-start = ((), (), s32[]{:S(2)}) async-start(), calls=%async_computation.3 | async-start | bytes 4456448 | tf_op jit(solution)/shard_map/all_gather | solution.py:22
  195.5 162.9 %all-reduce.10.cloned.1.call-start = ((), (), s32[]{:S(2)}) async-start(), calls=%async_computation.5 | async-start | bytes 8388608 | tf_op jit(solution)/shard_map/psum | solution.py:75
  195.7 32.2 %copy-start = (f32[16,1,128,512]{3,2,1,0:T(8,128)S(1)}, f32[16,1,128,512]{3,2,1,0:T(8,128)}, u32[]{:S(2)}) copy-start(f32[16,1,128,512]{3,2,1,0:T(8,128)} %param.3) | copy-start | bytes 12582916
  254.7 275.0 %all-reduce.8.cloned.1.call-start = ((), (), s32[]{:S(2)}) async-start(), calls=%async_computation.4 | async-start | bytes 10485760 | tf_op jit(solution)/shard_map/psum | solution.py:9
  358.4 5.4 copy-start.3
  532.5 1.6 copy-start.4
  532.5 1.8 copy-start.5
  532.5 6.6 %copy-start.2 = (f32[2048,512]{1,0:T(8,128)S(1)}, f32[2048,512]{1,0:T(8,128)}, u32[]{:S(2)}) copy-start(f32[2048,512]{1,0:T(8,128)} %all-gather.3.cloned.1.call-done) | copy-start | bytes 12582916
  533.1 6.0 %copy-start.1 = (f32[16,1,128,512]{3,2,1,0:T(8,128)S(1)}, f32[16,1,128,512]{3,2,1,0:T(8,128)}, u32[]{:S(2)}) copy-start(f32[16,1,128,512]{3,2,1,0:T(8,128)} %param.3) | copy-start | bytes 12582916
  534.3 12.4 %slice-start = ((s8[8388608]{0:T(1024)(128)(4,1)}), s8[4194304]{0:T(1024)(128)(4,1)S(1)}, s32[]{:S(2)}) async-start(s8[8388608]{0:T(1024)(128)(4,1)} %bitcast.61), calls=%async_computation.6 | async-start | bytes 8388608
  539.1 7.6 %slice-start.1 = ((s8[8388608]{0:T(1024)(128)(4,1)}), s8[4194304]{0:T(1024)(128)(4,1)S(1)}, s32[]{:S(2)}) async-start(s8[8388608]{0:T(1024)(128)(4,1)} %bitcast.61), calls=%async_computation.7 | async-start | bytes 8388608
  539.1 7.6 %copy-start.6 = (f32[1024,512]{1,0:T(8,128)S(1)}, f32[1024,512]{1,0:T(8,128)}, u32[]{:S(2)}) copy-start(f32[1024,512]{1,0:T(8,128)} %multiply_subtract_fusion) | copy-start | bytes 6291460
Sparse Core Ops, SparseCore 0:
  9.9 84.9 all-reduce.5
  114.6 80.7 reduce-scatter.1
  197.9 53.5 all-gather.2
  254.8 103.4 all-reduce.9
  368.6 161.1 all-reduce.7
where the time goes:
time: 602 us; the launch traced here: 596 us
  waiting for transfers between devices  434 us (72%)
  matrix products  90.1 us (15%)
  other arithmetic  46.9 us (8%)
  between operations  13.5 us (2%)
  local copies, waits for them, and re-layouts  10.6 us (2%)
    psum x2, waiting for transfers between devices, from_root(): return lax.psum(kept, axis)  246 us
    psum x1, waiting for transfers between devices, per_device(): direct = lax.psum(direct_part, 'col')  103 us
    reduce_scatter x1, waiting for transfers between devices, sum_by_parts(): lax.psum_scatter(rows_for(lines, lax.axis_size(axis)), axis, scatter_dime...  80.9 us
    dot_general x1, matrix products, per_device(): lax.dot_general(left_side, right_side, (((1,), (1,)), ((), ())), precisio...  33.6 us
    dot_general x3, matrix products, matmul(): jnp.dot(left_side, right_side, precision=lax.Precision.HIGHEST, preferred...  32.4 us
    select_n x1, other arithmetic, per_device(): direct_part = matmul(jnp.where(lower_mask, current, 0.0), refl_cols)  32.2 us
    dot_general x2, matrix products, inner(): lax.dot_general(left_side, right_side, (((0,), (0,)), ((), ())), precisio...  24.2 us
  transfers between devices with their start and end apart: 5, of which 5 were waited for; matrix products, arithmetic and copies ran while one was open for 9% of the time, Pallas kernels for 0%

commit v1 on v0

--- a/solution.py
+++ b/solution.py
@@ -6,7 +6,7 @@
 
 def from_root(value, axis, source):
     kept = jnp.where(lax.axis_index(axis) == source, value, 0).astype(value.dtype)
-    return lax.psum(kept, axis)
+    return jnp.sum(lax.all_gather(kept, axis), axis=0)
 
 
 def rows_for(lines, peers):

time: 602 us -> 1210 us (2.01)
  waiting for transfers between devices: 434 us -> 986 us
  other arithmetic: 46.9 us -> 91.8 us
    all_gather x0 -> x4, waiting for transfers between devices: none -> 644 us  [from_root(): return jnp.sum(lax.all_gather(kept, axis), axis=0)]
    psum x2 -> x1, waiting for transfers between devices: 246 us -> 132 us  [per_device(): projection = lax.psum(inner(refl_rows, w_rows), 'row')]
    all_gather x1, waiting for transfers between devices: 3.54 us -> 56 us  [sum_by_parts(): whole = lax.all_gather(own, axis).reshape(-1, *lines.shape[1:])]
    reduce_sum x0 -> x4, other arithmetic: none -> 45.3 us  [from_root(): return jnp.sum(lax.all_gather(kept, axis), axis=0)]
    psum x1, waiting for transfers between devices: 103 us -> 74.1 us  [per_device(): direct = lax.psum(direct_part, 'col')]
  transfers between devices with their start and end apart: 5 -> 8, of which waited for: 5 -> 8; matrix products, arithmetic and copies ran while one was open for 9% -> 7% of each run, Pallas kernels for 0% -> 0%
where the time goes in v1:
time: 1210 us; the launch traced here: 1200 us
  waiting for transfers between devices  986 us (81%)
  other arithmetic  91.8 us (8%)
  matrix products  91.7 us (8%)
  between operations  14 us (1%)
    all_gather x4, waiting for transfers between devices, from_root(): return jnp.sum(lax.all_gather(kept, axis), axis=0)  644 us
    psum x1, waiting for transfers between devices, per_device(): projection = lax.psum(inner(refl_rows, w_rows), 'row')  132 us
    reduce_scatter x1, waiting for transfers between devices, sum_by_parts(): lax.psum_scatter(rows_for(lines, lax.axis_size(axis)), axis, scatter_dime...  79.4 us
    psum x1, waiting for transfers between devices, per_device(): direct = lax.psum(direct_part, 'col')  74.1 us
    all_gather x1, waiting for transfers between devices, sum_by_parts(): whole = lax.all_gather(own, axis).reshape(-1, *lines.shape[1:])  56 us
    reduce_sum x4, other arithmetic, from_root(): return jnp.sum(lax.all_gather(kept, axis), axis=0)  45.3 us
    dot_general x3, matrix products, matmul(): jnp.dot(left_side, right_side, precision=lax.Precision.HIGHEST, preferred...  33.7 us
    dot_general x1, matrix products, per_device(): lax.dot_general(left_side, right_side, (((1,), (1,)), ((), ())), precisio...  33.5 us
  transfers between devices with their start and end apart: 8, of which 8 were waited for; matrix products, arithmetic and copies ran while one was open for 7% of the time, Pallas kernels for 0%

profile of v1, /device:TPU:0, one launch (start us, length us, event | category | flops | bytes accessed | tf_op | source)
XLA Modules:
  0.0 1203.3 jit_solution(10605724246177749451)
XLA Ops:
  6.5 3.2 dynamic-slice_select_fusion.1
  10.0 173.1 %all-gather.9.cloned.1.call-done = f32[8,1024,512]{2,1,0:T(8,128)} async-done(((f32[1,1024,512]{2,1,0:T(8,128)}), f32[8,1024,512]{2,1,0:T(8,128)}) %all-gather.9.cloned.1.call-update) | async-done | bytes 16777232 | tf_op jit(solution)/shard_map/all_gather | solution.py:9
  183.1 8.1 reduce_sum.36
  191.2 19.8 %fusion.4 = f32[2048,512]{1,0:T(8,128)} fusion(f32[1024,512]{1,0:T(8,128)S(1)} %reduce_sum.36, f32[128,8,16,128]{3,2,1,0:T(8,128)} %bitcast.60, s32[2048]{0:T(1024)S(1)} %get-tuple-element.11, s32[1024]{0:T(1024)S(1)} %get-tuple-element.9), kind=kOutput, calls=%fused_computation.7 | convolution fusion | flops 12889096192 | bytes 14692352 | tf_op jit(solution)/shard_map/dot_general | solution.py:64
  211.1 79.4 %reduce-scatter.2.cloned.1.call-done = f32[128,512]{1,0:T(8,128)} async-done(((f32[2048,512]{1,0:T(8,128)}), f32[128,512]{1,0:T(8,128)}) %reduce-scatter.2.cloned.1.call-update) | async-done | bytes 262160 | tf_op jit(solution)/shard_map/reduce_scatter | solution.py:19
  290.6 56.0 %all-gather.13.cloned.1.call-done = f32[2048,512]{1,0:T(8,128)} async-done(((f32[128,512]{1,0:T(8,128)}), f32[2048,512]{1,0:T(8,128)}) %all-gather.13.cloned.1.call-update) | async-done | bytes 4194320 | tf_op jit(solution)/shard_map/all_gather | solution.py:22
  346.6 3.2 dynamic-slice_select_fusion
  350.1 32.2 %fusion = f32[8,128,16,128]{3,2,1,0:T(8,128)} fusion(f32[8,1,128,16,1,128]{5,4,3,2,1,0:T(1,128)} %param.2, s32[16,128]{1,0:T(8,128)S(1)} %get-tuple-element.10, s32[8,128]{1,0:T(8,128)S(1)} %get-tuple-element.8), kind=kLoop, calls=%fused_computation.1 | loop fusion | flops 4194304 | bytes 16789504 | tf_op jit(solution)/shard_map/jit(_where)/select_n | solution.py:73
  382.3 19.5 %fusion.1 = f32[1024,512]{1,0:T(8,128)} fusion(f32[2048,512]{1,0:T(8,128)S(1)} %bitcast.54, f32[128,8,16,128]{3,2,1,0:T(8,128)} %bitcast.64), kind=kOutput, calls=%fused_computation.2 | convolution fusion | flops 12884901888 | bytes 14680064 | tf_op jit(solution)/shard_map/dot_general | solution.py:56
  401.9 116.7 %all-gather.11.cloned.1.call-done = f32[8,1024,512]{2,1,0:T(8,128)} async-done(((f32[1,1024,512]{2,1,0:T(8,128)}), f32[8,1024,512]{2,1,0:T(8,128)}) %all-gather.11.cloned.1.call-update) | async-done | bytes 16777232 | tf_op jit(solution)/shard_map/all_gather | solution.py:9
  518.6 9.4 reduce_sum.37
  528.0 74.1 %all-reduce.3.cloned.1.call-done = f32[1024,512]{1,0:T(8,128)} async-done(((f32[1024,512]{1,0:T(8,128)}), f32[1024,512]{1,0:T(8,128)}) %all-reduce.3.cloned.1.call-update) | async-done | bytes 2097168 | tf_op jit(solution)/shard_map/psum | solution.py:75
  602.1 5.4 fusion.27
  607.5 4.7 fusion.28
  613.0 8.8 all-gather.15.cloned.1.call-start
  621.8 132.1 %all-reduce.5.cloned.1.call-done = f32[512,512]{1,0:T(8,128)} async-done(((f32[512,512]{1,0:T(8,128)}), f32[512,512]{1,0:T(8,128)}) %all-reduce.5.cloned.1.call-update) | async-done | bytes 1048592 | tf_op jit(solution)/shard_map/psum | solution.py:84
  753.8 6.7 multiply_subtract_fusion
  760.5 182.1 %all-gather.17.cloned.1.call-done = f32[16384,512]{1,0:T(8,128)} async-done(((f32[1024,512]{1,0:T(8,128)}), f32[16384,512]{1,0:T(8,128)}) %all-gather.17.cloned.1.call-update) | async-done | bytes 33554448 | tf_op jit(solution)/shard_map/all_gather | solution.py:9
  942.6 13.8 %reduce_sum.39 = f32[1024,512]{1,0:T(8,128)S(1)} reduce(f32[16,1024,512]{2,1,0:T(8,128)} %bitcast.51, f32[]{:T(128)} %constant.57.clone.1), dimensions={0}, to_apply=%region_6.7 | reduce | flops 7864320 | bytes 35651588 | tf_op jit(solution)/shard_map/reduce_sum | solution.py:9
  956.4 171.7 %all-gather.15.cloned.1.call-done = f32[16384,512]{1,0:T(8,128)} async-done(((f32[1024,512]{1,0:T(8,128)}), f32[16384,512]{1,0:T(8,128)}) %all-gather.15.cloned.1.call-update) | async-done | bytes 33554448 | tf_op jit(solution)/shard_map/all_gather | solution.py:9
  1128.0 14.1 %reduce_sum.38 = f32[1024,512]{1,0:T(8,128)} reduce(f32[16,1024,512]{2,1,0:T(8,128)} %bitcast.52, f32[]{:T(128)} %constant.57.clone.1), dimensions={0}, to_apply=%region_5.6 | reduce | flops 7864320 | bytes 35651588 | tf_op jit(solution)/shard_map/reduce_sum | solution.py:9
  1146.2 7.5 bitcast_subtract_fusion.1
  1153.8 33.5 %fusion.6 = f32[128,8,16,128]{3,1,2,0:T(8,128)} fusion(f32[128,8,16,128]{3,2,1,0:T(8,128)S(1)} %bitcast.63, s32[2048]{0:T(1024)S(1)} %get-tuple-element.11, s32[1024]{0:T(1024)S(1)} %get-tuple-element.9, f32[2048,512]{1,0:T(8,128)S(1)} %bitcast.56, f32[2048,512]{1,0:T(8,128)S(1)} %bitcast_subtract_fusion.1, f32[1024,512]{1,0:T(8,128)S(1)} %copy-done.7, ...), kind=kOutput, calls=%fused_computation.9 | convolution fusion | flops 25779240960 | bytes 29372416 | tf_op jit(solution)/shard_map/dot_general | solution.py:89
  1187.3 8.8 copy.7
  (41 shorter events, 5.6 us)
Async XLA Ops:
  6.5 176.6 %all-gather.9.cloned.1.call-start = ((), (), s32[]{:S(2)}) async-start(), calls=%async_computation.1 | async-start | bytes 18874368 | tf_op jit(solution)/shard_map/all_gather | solution.py:9
  9.8 280.7 %reduce-scatter.2.cloned.1.call-start = ((), (), s32[]{:S(2)}) async-start(), calls=%async_computation.3 | async-start | bytes 4456448 | tf_op jit(solution)/shard_map/reduce_scatter | solution.py:19
  191.2 19.8 %copy-start = (f32[1024,512]{1,0:T(8,128)}, f32[1024,512]{1,0:T(8,128)S(1)}, u32[]{:S(2)}) copy-start(f32[1024,512]{1,0:T(8,128)S(1)} %reduce_sum.36) | copy-start | bytes 6291460
  211.0 135.5 %all-gather.13.cloned.1.call-start = ((), (), s32[]{:S(2)}) async-start(), calls=%async_computation.6 | async-start | bytes 4456448 | tf_op jit(solution)/shard_map/all_gather | solution.py:22
  290.5 228.0 %all-gather.11.cloned.1.call-start = ((), (), s32[]{:S(2)}) async-start(), calls=%async_computation.4 | async-start | bytes 18874368 | tf_op jit(solution)/shard_map/all_gather | solution.py:9
  349.8 252.3 %all-reduce.3.cloned.1.call-start = ((), (), s32[]{:S(2)}) async-start(), calls=%async_computation.2 | async-start | bytes 4194304 | tf_op jit(solution)/shard_map/psum | solution.py:75
  350.1 32.2 %copy-start.3 = (f32[16,1,128,512]{3,2,1,0:T(8,128)S(1)}, f32[16,1,128,512]{3,2,1,0:T(8,128)}, u32[]{:S(2)}) copy-start(f32[16,1,128,512]{3,2,1,0:T(8,128)} %param.3) | copy-start | bytes 12582916
  401.9 352.0 %all-reduce.5.cloned.1.call-start = ((), (), s32[]{:S(2)}) async-start(), calls=%async_computation.5 | async-start | bytes 2097152 | tf_op jit(solution)/shard_map/psum | solution.py:84
  602.1 5.4 copy-start.1
  612.2 330.4 %all-gather.17.cloned.1.call-start = ((), (), s32[]{:S(2)}) async-start(), calls=%async_computation.8 | async-start | bytes 35651584 | tf_op jit(solution)/shard_map/all_gather | solution.py:9
  613.0 515.1 %all-gather.15.cloned.1.call-start = ((), (), s32[]{:S(2)}) async-start(), calls=%async_computation.7 | async-start | bytes 35651584 | tf_op jit(solution)/shard_map/all_gather | solution.py:9
  1128.0 16.3 %copy-start.6 = (f32[512,512]{1,0:T(8,128)S(1)}, f32[512,512]{1,0:T(8,128)}, u32[]{:S(2)}) copy-start(f32[512,512]{1,0:T(8,128)} %all-reduce.5.cloned.1.call-done) | copy-start | bytes 3145732
  1142.1 2.8 copy-start.4
  1142.1 4.1 copy-start.5
  1142.1 11.6 slice-start
  1146.2 7.6 copy-start.2
  1146.2 7.6 slice-start.1
  1146.2 7.6 copy-start.7
Sparse Core Ops, SparseCore 0:
  9.9 173.1 all-gather.8
  211.2 79.3 reduce-scatter.1
  293.0 53.5 all-gather.12
  349.9 168.5 all-gather.10
  520.9 81.0 all-reduce.2
  612.3 141.4 all-reduce.4
  756.3 186.2 all-gather.16
  945.1 182.9 all-gather.14
